TPU v7x, 32 devices: a whole 2x2x4 slice. The times are simulated.
32 devices in a mesh: feat: 8 (over z, y), samp: 4 (over x, core).
Axes of the slice: x: 2, y: 2, z: 4, core: 2. Of those that a mesh axis runs over, the one named last changes fastest.
Arguments:
- design: bfloat16 [14336, 8192], P('samp', 'feat'), may hold values from -0.0625 to 0.0625
- targets: bfloat16 [14336, 128], P('samp'), may hold values from -26 to 26
- warm_start: float32 [8192, 128], P('feat'), may hold values from -0.6 to 0.6
- active_mask: int32 [2, 8192], P(None, 'feat'), may hold values 0 or 1
- penalty_index: int32 [1], replicated, may hold values from 0 to 7
Outputs:
- coefficients: float32 [8192, 128], P('feat')
- correlations: float32 [3, 8192], P(None, 'feat')
- relative_gaps: float32 [3], replicated
- pruned_counts: float32 [2], replicated
All inputs are finite; a program needn't handle non-finite values. No bound on the sum of `active_mask` on one device may be relied on, other than what follows from the above.
Results may differ from a plain program's by a relative error of at most 0.0024.
The roundings to bfloat16 on the way count: a program that leaves them out, or rounds other values in their place, can miss the bound.
Values may be sent and summed in bfloat16 or wider, within the bound.
A program may use at most 64 MiB of HBM per device.

v0:
```python
import jax
import jax.numpy as jnp
from jax import lax
from jax.sharding import PartitionSpec as P

ITERS = 2


def group_norms(matrix):
    return jnp.sqrt(jnp.sum(matrix * matrix, axis=1))


def transpose_product(design, right_side):
    return lax.dot_general(
        design, right_side, (((0,), (0,)), ((), ())), preferred_element_type=jnp.float32
    )


def local(design, targets, warm_start, active_mask, penalty_index):
    row_count, col_count = design.shape
    feat_size = lax.axis_size("feat")
    feat_slot = lax.axis_index("feat")
    block_rows = row_count // feat_size
    samp_first = (lax.axis_index("samp") == 0).astype(jnp.float32)
    corr_local = transpose_product(design, targets)
    squares_local = jnp.sum(jnp.square(design.astype(jnp.float32)), axis=0)
    corr_y, column_squares = lax.psum((corr_local, squares_local), "samp")
    penalty_max = lax.pmax(jnp.max(group_norms(corr_y)), "feat")
    penalty = penalty_max / (8.0 + 4.0 * penalty_index[0].astype(jnp.float32))
    step_sizes = 0.5 / (1.0 + column_squares)
    current = warm_start
    correlations = []
    relative_gaps = []
    pruned_counts = []
    own_targets = lax.dynamic_slice_in_dim(targets, feat_slot * block_rows, block_rows, 0)
    for iteration in range(ITERS + 1):
        current_half = current.astype(jnp.bfloat16)
        fitted_part = jnp.dot(design, current_half, preferred_element_type=jnp.float32)
        fitted = lax.psum(fitted_part, "feat")
        residual_all = (targets.astype(jnp.float32) - fitted).astype(jnp.bfloat16)
        residual = lax.dynamic_slice_in_dim(residual_all, feat_slot * block_rows, block_rows, 0)
        grad_local = transpose_product(design, residual_all)
        resid_float = residual.astype(jnp.float32)
        rr_local = jnp.sum(resid_float * resid_float)
        ry_local = jnp.sum(resid_float * own_targets.astype(jnp.float32))
        bn_local = samp_first * jnp.sum(group_norms(current))
        if iteration < ITERS:
            keep = active_mask[iteration].astype(jnp.float32)
            pruned_local = samp_first * jnp.sum(1.0 - keep)
        else:
            pruned_local = jnp.zeros((), jnp.float32)
        gradient = lax.psum(grad_local, "samp")
        grad_norms = group_norms(gradient)
        local_max = jnp.max(grad_norms)
        grad_top = lax.pmax(local_max, "feat")
        rr_sum, ry_sum, bn_sum, pruned_sum = lax.psum(
            (rr_local, ry_local, bn_local, pruned_local), ("feat", "samp")
        )
        scale = jnp.maximum(penalty, grad_top)
        correlations.append(grad_norms / scale)
        primal = 0.5 * rr_sum + penalty * bn_sum
        ratio = penalty / scale
        dual = ratio * ry_sum - 0.5 * ratio * ratio * rr_sum
        relative_gaps.append((primal - dual) / (primal + 1.0))
        if iteration < ITERS:
            pruned_counts.append(pruned_sum)
            moved = current + step_sizes[:, None] * gradient
            moved_norms = group_norms(moved)
            cutoff = step_sizes * penalty
            factor = jnp.maximum(moved_norms - cutoff, 0.0) / jnp.maximum(moved_norms, cutoff)
            current = (keep * factor)[:, None] * moved
    return (current, jnp.stack(correlations), jnp.stack(relative_gaps), jnp.stack(pruned_counts))


def solution(mesh):
    placed = (P("samp", "feat"), P("samp", None), P("feat", None), P(None, "feat"), P())
    return jax.shard_map(
        local,
        mesh=mesh,
        in_specs=placed,
        out_specs=(P("feat", None), P(None, "feat"), P(), P()),
        check_vma=False,
    )
```

profile of v0, /device:TPU:0, one launch (start us, length us, event | category | flops | bytes accessed | tf_op | source)
XLA Modules:
  0.0 527.3 jit_solution(8647449387170644454)
XLA Ops:
  7.2 6.5 %fusion.5 = f32[3584,128]{1,0:T(8,128)} fusion(bf16[3584,1024]{1,0:T(8,128)(2,1)} %param.5, f32[1024,128]{1,0:T(8,128)} %param.7), kind=kOutput, calls=%fused_computation.33 | convolution fusion | flops 939655168 | bytes 9699328 | tf_op jit(solution)/shard_map/dot_general | solution.py:38
  13.8 6.0 %fusion.13 = f32[1024,128]{1,0:T(8,128)} fusion(bf16[3584,1024]{1,0:T(8,128)(2,1)} %param.5, bf16[3584,128]{1,0:T(8,128)(2,1)S(1)} %copy-done), kind=kOutput, calls=%fused_computation.61 | convolution fusion | flops 939524096 | bytes 8781824 | tf_op jit(solution)/shard_map/dot_general | solution.py:14
  19.8 92.7 %all-reduce.10.cloned.1.call-done = f32[3584,128]{1,0:T(8,128)} async-done(((f32[3584,128]{1,0:T(8,128)}), f32[3584,128]{1,0:T(8,128)}) %all-reduce.10.cloned.1.call-update) | async-done | bytes 1835024 | tf_op jit(solution)/shard_map/psum | solution.py:39
  112.5 1.7 fusion
  114.1 5.0 convolution_bitcast_fusion.4
  119.3 4.6 multiply_reduce_fusion
  125.5 7.1 %psum.133 = f32[1024]{0:T(1024)S(1)} all-reduce(f32[1024]{0:T(1024)S(1)} %multiply_reduce_fusion), channel_id=1, replica_groups=mesh['feat'=8,'samp'=4] {'samp'}, use_global_device_ids=true, to_apply=%region_1.0 | all-reduce | flops 1024 | bytes 8192 | tf_op jit(solution)/shard_map/psum | solution.py:27
  132.7 22.5 %all-reduce.20.cloned.1.call-done = (f32[1024,128]{0,1:T(8,128)}, f32[1024,128]{1,0:T(8,128)}) async-done(((f32[1024,128]{0,1:T(8,128)}, f32[1024,128]{1,0:T(8,128)}), (f32[1024,128]{0,1:T(8,128)}, f32[1024,128]{1,0:T(8,128)})) %all-reduce.20.cloned.1.call-update) | async-done | bytes 1048592 | tf_op jit(solution)/shard_map/psum | solution.py:52
  155.2 1.2 multiply_reduce_fusion.8
  157.1 22.0 %pmax.28 = f32[]{:T(128)} all-reduce(f32[]{:T(128)} %sqrt_reduce_fusion.3), channel_id=1, replica_groups=mesh['feat'=8,'samp'=4] {'feat'}, use_global_device_ids=true, to_apply=%region_8.0 | all-reduce | flops 1 | bytes 8 | tf_op jit(solution)/shard_map/pmax | solution.py:28
  179.7 1.3 multiply_reduce_fusion.9
  181.7 6.4 %convolution_bitcast_fusion.1 = f32[3584,128]{1,0:T(8,128)} fusion(bf16[3584,1024]{1,0:T(8,128)(2,1)} %param.5, f32[1024,128]{0,1:T(8,128)S(1)} %get-tuple-element.36, f32[1024]{0:T(1024)S(1)} %get-tuple-element.41), kind=kOutput, calls=%fused_computation.2 | convolution fusion | flops 939786240 | bytes 9703424 | tf_op jit(solution)/shard_map/dot_general | solution.py:38
  188.1 92.7 %all-reduce.12.cloned.1.call-done = f32[3584,128]{1,0:T(8,128)} async-done(((f32[3584,128]{1,0:T(8,128)}), f32[3584,128]{1,0:T(8,128)}) %all-reduce.12.cloned.1.call-update) | async-done | bytes 1835024 | tf_op jit(solution)/shard_map/psum | solution.py:39
  280.9 1.7 fusion.1
  282.6 5.0 convolution_bitcast_fusion.3
  287.8 32.8 %all-reduce.14.cloned.1.call-done = f32[1024,128]{0,1:T(8,128)} async-done(((f32[1024,128]{0,1:T(8,128)}), f32[1024,128]{0,1:T(8,128)}) %all-reduce.14.cloned.1.call-update) | async-done | bytes 524304 | tf_op jit(solution)/shard_map/psum | solution.py:52
  324.5 6.4 %convolution_bitcast_fusion = f32[3584,128]{1,0:T(8,128)} fusion(bf16[3584,1024]{1,0:T(8,128)(2,1)} %param.5, f32[1024,128]{0,1:T(8,128)S(1)} %get-tuple-element.34), kind=kOutput, calls=%fused_computation.1 | convolution fusion | flops 939655168 | bytes 9699328 | tf_op jit(solution)/shard_map/dot_general | solution.py:38
  334.3 92.8 %all-reduce.16.cloned.1.call-done = f32[3584,128]{1,0:T(8,128)} async-done(((f32[3584,128]{1,0:T(8,128)}), f32[3584,128]{1,0:T(8,128)}) %all-reduce.16.cloned.1.call-update) | async-done | bytes 1835024 | tf_op jit(solution)/shard_map/psum | solution.py:39
  427.1 1.7 fusion.2
  429.7 5.1 convolution_bitcast_fusion.2
  439.0 1.7 fusion.10
  440.7 41.8 %all-reduce = (f32[]{:T(128)}, f32[]{:T(128)}, f32[]{:T(128)}, f32[]{:T(128)}, f32[]{:T(128)}, /*index=5*/f32[]{:T(128)}, f32[]{:T(128)}, f32[]{:T(128)}, f32[]{:T(128)}, f32[1]{0:T(128)}, /*index=10*/f32[1]{0:T(128)}) all-reduce(f32[]{:T(128)} %get-tuple-element.12, ...), channel_id=1, replica_groups=mesh['feat'=8,'samp'=4] {'feat','samp'}, use_global_device_ids=true, to_apply=%region_38.0 | all-reduce | flops 11 | bytes 88 | tf_op jit(solution)/shard_map/psum | solution.py:56
  486.2 1.9 pad_maximum_fusion.2
  489.9 21.7 %all-reduce.1 = (f32[]{:T(128)}, f32[]{:T(128)}, f32[]{:T(128)}) all-reduce(f32[]{:T(128)} %sqrt_reduce_fusion.4, f32[]{:T(128)} %sqrt_reduce_fusion.5, f32[]{:T(128)} %sqrt_reduce_fusion.6), channel_id=1, replica_groups=mesh['feat'=8,'samp'=4] {'feat'}, use_global_device_ids=true, to_apply=%region_22.0 | all-reduce | flops 3 | bytes 24 | tf_op jit(solution)/shard_map/pmax | solution.py:55
  (49 shorter events, 14.8 us)
Async XLA Ops:
  7.2 6.6 %copy-start = (bf16[3584,128]{1,0:T(8,128)(2,1)S(1)}, bf16[3584,128]{1,0:T(8,128)(2,1)}, u32[]{:S(2)}) copy-start(bf16[3584,128]{1,0:T(8,128)(2,1)} %param.6) | copy-start | bytes 2752516
  7.2 105.3 %all-reduce.10.cloned.1.call-start = ((), (), s32[]{:S(2)}) async-start(), calls=%async_computation | async-start | bytes 3670016 | tf_op jit(solution)/shard_map/psum | solution.py:39
  13.7 141.5 %all-reduce.20.cloned.1.call-start = ((), (), s32[]{:S(2)}) async-start(), calls=%async_computation.5 | async-start | bytes 2097152 | tf_op jit(solution)/shard_map/psum | solution.py:52
  119.2 4.7 copy-start.4
  119.2 13.5 %copy-start.6 = (s32[2,1024]{1,0:T(2,128)S(1)}, s32[2,1024]{1,0:T(2,128)}, u32[]{:S(2)}) copy-start(s32[2,1024]{1,0:T(2,128)} %param.8) | copy-start | bytes 24580
  119.2 161.7 %all-reduce.12.cloned.1.call-start = ((), (), s32[]{:S(2)}) async-start(), calls=%async_computation.1 | async-start | bytes 3670016 | tf_op jit(solution)/shard_map/psum | solution.py:39
  188.1 132.6 %all-reduce.14.cloned.1.call-start = ((), (), s32[]{:S(2)}) async-start(), calls=%async_computation.2 | async-start | bytes 1048576 | tf_op jit(solution)/shard_map/psum | solution.py:52
  287.6 139.5 %all-reduce.16.cloned.1.call-start = ((), (), s32[]{:S(2)}) async-start(), calls=%async_computation.3 | async-start | bytes 3670016 | tf_op jit(solution)/shard_map/psum | solution.py:39
  323.7 0.8 copy-start.2
  323.8 7.3 %copy-start.5 = (f32[1024,128]{1,0:T(8,128)S(1)}, f32[1024,128]{1,0:T(8,128)}, u32[]{:S(2)}) copy-start(f32[1024,128]{1,0:T(8,128)} %param.7) | copy-start | bytes 1572868
  331.0 157.1 %all-reduce.18.cloned.1.call-start = ((), (), s32[]{:S(2)}) async-start(), calls=%async_computation.4 | async-start | bytes 1048576 | tf_op jit(solution)/shard_map/psum | solution.py:52
  428.7 0.9 copy-start.1
  429.7 5.8 %copy-start.3 = (f32[1024,128]{0,1:T(8,128)S(1)}, f32[1024,128]{0,1:T(8,128)}, u32[]{:S(2)}) copy-start(f32[1024,128]{0,1:T(8,128)} %copy-done.2) | copy-start | bytes 1572868
Sparse Core Ops, SparseCore 0:
  13.9 98.5 all-reduce.9
  119.3 35.8 all-reduce.19
  188.2 92.6 all-reduce.11
  287.7 32.9 all-reduce.13
  331.1 95.9 all-reduce.15
  434.9 33.1 all-reduce.17
where the time goes:
time: 528 us; the launch traced here: 527 us
  waiting for transfers between devices  334 us (63%)
  blocking collectives  92.5 us (18%)
  matrix products  40.5 us (8%)
  between operations  30.1 us (6%)
  other arithmetic  26.4 us (5%)
    psum x3, waiting for transfers between devices, local(): fitted = lax.psum(fitted_part, 'feat')  278 us
    psum x3, waiting for transfers between devices, local(): gradient = lax.psum(grad_local, 'samp')  55.4 us
    psum x1, blocking collectives, local(): lax.psum((rr_local, ry_local, bn_local, pruned_local), ('feat', 'samp'))  41.8 us
    pmax x1, blocking collectives, local(): penalty_max = lax.pmax(jnp.max(group_norms(corr_y)), 'feat')  22 us
    pmax x1, blocking collectives, local(): grad_top = lax.pmax(local_max, 'feat')  21.7 us
    dot_general x4, matrix products, transpose_product(): lax.dot_general(design, right_side, (((0,), (0,)), ((), ())), preferred_e...  21.2 us
    dot_general x3, matrix products, local(): jnp.dot(design, current_half, preferred_element_type=jnp.float32)  19.3 us
  transfers between devices with their start and end apart: 6, of which 5 were waited for; matrix products, arithmetic and copies ran while one was open for 4% of the time, Pallas kernels for 0%

commit v1 on v0

--- a/solution.py
+++ b/solution.py
@@ -1,9 +1,394 @@
+import functools
+
 import jax
 import jax.numpy as jnp
 from jax import lax
+from jax.experimental import pallas as pl
+from jax.experimental.pallas import tpu as pltpu
 from jax.sharding import PartitionSpec as P
 
 ITERS = 2
+F32 = jnp.float32
+BF16 = jnp.bfloat16
+LANES = 128
+SHARE = BF16
+GRAD = F32
+STATS = 16
+
+
+def fold(row, combine):
+    pieces = [row[:, at : at + LANES] for at in range(0, row.shape[1], LANES)]
+    return functools.reduce(combine, pieces)
+
+
+def top(matrix):
+    return jnp.max(jnp.max(matrix, axis=0, keepdims=True), axis=1, keepdims=True)
+
+
+def total_of(matrix):
+    return jnp.sum(jnp.sum(matrix, axis=0, keepdims=True), axis=1, keepdims=True)
+
+
+def column_norms(matrix):
+    return jnp.sqrt(jnp.sum(matrix * matrix, axis=0, keepdims=True))
+
+
+def kernel(
+    sizes, design, targets, warm, mask, index, coef_out, corr_out, info_out,
+    mine, ysend, yrecv, zsend, zrecv, resid, turned, gsend, grecv, half, cur, squares,
+    sqrecv, coefs, norms, exf, exs,
+    y_s, y_r, z_s, z_r, a_s, a_r, b_s, b_r, g_s, g_r, h_s, h_r, q_s, q_r, c_s, c_r, n_s, n_r,
+    ef_s, ef_r, es_s, es_r,
+):
+    F, Z, S = sizes
+    R, C = design.shape
+    K = targets.shape[1]
+    B = R // F
+    W = C // S
+    f = lax.axis_index("feat")
+    s = lax.axis_index("samp")
+    z, y = f // 2, lax.rem(f, 2)
+    partner = z * 2 + 1 - y
+
+    def ahead_z(off):
+        return lax.rem(z + off, Z)
+
+    def behind_z(off):
+        return lax.rem(z - off + Z, Z)
+
+    def ahead_s(off):
+        return lax.rem(s + off, S)
+
+    def feat_copy(src, dst, send, recv, to):
+        return pltpu.make_async_remote_copy(
+            src_ref=src, dst_ref=dst, send_sem=send, recv_sem=recv,
+            device_id={"feat": to}, device_id_type=pl.DeviceIdType.MESH,
+        )
+
+    def samp_copy(src, dst, send, recv, off):
+        return pltpu.make_async_remote_copy(
+            src_ref=src, dst_ref=dst, send_sem=send, recv_sem=recv,
+            device_id={"samp": ahead_s(off)}, device_id_type=pl.DeviceIdType.MESH,
+        )
+
+    def copy_y(t, off):
+        return feat_copy(ysend.at[t, off], yrecv.at[t, off], y_s.at[t, off], y_r.at[t, off], partner)
+
+    def copy_z(t, off):
+        return feat_copy(
+            zsend.at[t, off], zrecv.at[t, off], z_s.at[t, off], z_r.at[t, off], ahead_z(off) * 2 + y
+        )
+
+    def copy_a(t, off):
+        return feat_copy(
+            resid.at[t, f], resid.at[t, f], a_s.at[t, off], a_r.at[t, off], ahead_z(off) * 2 + y
+        )
+
+    def copy_b(t, off):
+        slot = behind_z(off) * 2 + y
+        return feat_copy(resid.at[t, slot], resid.at[t, slot], b_s.at[t, off], b_r.at[t, off], partner)
+
+    def copy_g(t, off):
+        return samp_copy(gsend.at[t, off], grecv.at[t, off], g_s.at[t, off], g_r.at[t, off], off)
+
+    def copy_h(t, off):
+        return samp_copy(half.at[t, s], half.at[t, s], h_s.at[t, off], h_r.at[t, off], off)
+
+    def copy_q(off):
+        return samp_copy(squares.at[ahead_s(off)], sqrecv.at[off], q_s.at[off], q_r.at[off], off)
+
+    def copy_c(off):
+        return samp_copy(coefs.at[s], coefs.at[s], c_s.at[off], c_r.at[off], off)
+
+    def copy_n(off):
+        return samp_copy(norms.at[s], norms.at[s], n_s.at[off], n_r.at[off], off)
+
+    def copy_ef(e, off):
+        return feat_copy(
+            exf.at[e, f], exf.at[e, f], ef_s.at[e, off], ef_r.at[e, off], lax.rem(f + off, F)
+        )
+
+    def copy_es(e, off):
+        return samp_copy(exs.at[e, s], exs.at[e, s], es_s.at[e, off], es_r.at[e, off], off)
+
+    def each(count, body, first=0):
+        def step(at, carry):
+            body(at)
+            return carry
+
+        lax.fori_loop(first, count, step, 0)
+
+    barrier = pltpu.get_barrier_semaphore()
+    for off in range(1, F):
+        pl.semaphore_signal(
+            barrier, inc=1, device_id={"feat": lax.rem(f + off, F)}, device_id_type=pl.DeviceIdType.MESH
+        )
+    for off in range(1, S):
+        pl.semaphore_signal(
+            barrier, inc=1, device_id={"samp": ahead_s(off)}, device_id_type=pl.DeviceIdType.MESH
+        )
+
+    half[0] = warm[...].astype(BF16).reshape(S, W, K)
+    norms[s] = jnp.zeros((8, W), F32)
+    cur[...] = warm[pl.ds(pl.multiple_of(s * W, W), W), :].T
+    pl.semaphore_wait(barrier, F - 1 + S - 1)
+
+    def rows_of(slot):
+        return pl.ds(pl.multiple_of(slot * B, B), B)
+
+    def share(t, slot):
+        return jnp.dot(design[rows_of(slot), :], half[t].reshape(C, K), preferred_element_type=F32)
+
+    def turn(source):
+        step = 2 * B
+        for k in range(Z):
+            turned[:, k * step : (k + 1) * step] = source(k).T
+
+    def grad_parts(t):
+        def part(off):
+            at = pl.ds(pl.multiple_of(ahead_s(off) * W, W), W)
+            return jnp.dot(turned[...], design[:, at], preferred_element_type=F32)
+
+        def send(off):
+            gsend[t, off] = part(off).astype(GRAD)
+            copy_g(t, off).start()
+
+        each(S, send, 1)
+        gsend_own = part(0)
+        return gsend_own
+
+    def grad_sum(t, own):
+        for off in range(1, S):
+            copy_g(t, off).wait_recv()
+            own = own + grecv[t, off].astype(F32)
+        return own
+
+    def square_columns():
+        tall = 16
+
+        def body(at, acc):
+            rows = design[pl.ds(pl.multiple_of(at * tall, tall), tall), :].astype(F32)
+            rows = rows * rows
+            return acc + rows[:8] + rows[8:]
+
+        acc = lax.fori_loop(0, R // tall, body, jnp.zeros((8, C), F32), unroll=4)
+        for c in range(S):
+            squares[c] = acc[:, c * W : (c + 1) * W]
+        for off in range(1, S):
+            copy_q(off).start()
+
+    sums = []
+    bn_rows, gmax_rows, pruned_rows = [], [], []
+    penalty = None
+    step_sizes = None
+    for t in range(ITERS + 1):
+        bn_rows.append(fold(column_norms(cur[...]), jnp.add))
+
+        def send_y(i):
+            off = lax.rem(i + 1, Z)
+            ysend[t, off] = share(t, ahead_z(off) * 2 + 1 - y).astype(SHARE)
+            copy_y(t, off).start()
+
+        each(Z, send_y)
+
+        def send_z(off):
+            mine[...] = share(t, ahead_z(off) * 2 + y)
+            copy_y(t, off).wait_recv()
+            zsend[t, off] = (mine[...] + yrecv[t, off].astype(F32)).astype(SHARE)
+            copy_z(t, off).start()
+
+        each(Z, send_z, 1)
+        mine[...] = share(t, f)
+        if t == 0:
+            turn(lambda k: targets[k * 2 * B : (k + 1) * 2 * B, :])
+            corr_own = grad_parts(ITERS + 1)
+            square_columns()
+        copy_y(t, 0).wait_recv()
+        fitted = mine[...] + yrecv[t, 0].astype(F32)
+        for off in range(1, Z):
+            copy_z(t, off).wait_recv()
+            fitted = fitted + zrecv[t, off].astype(F32)
+        own_targets = targets[rows_of(f), :].astype(F32)
+        rounded = (own_targets - fitted).astype(BF16)
+        resid[t, f] = rounded
+        for off in range(1, Z):
+            copy_a(t, off).start()
+        copy_b(t, 0).start()
+        wide = rounded.astype(F32)
+        sums.append(
+            (
+                jnp.sum(wide * wide, axis=0, keepdims=True),
+                jnp.sum(wide * own_targets, axis=0, keepdims=True),
+            )
+        )
+        if t == 0:
+            corr = grad_sum(ITERS + 1, corr_own)
+            exf[0, f] = jnp.broadcast_to(fold(column_norms(corr), jnp.maximum), (STATS, LANES))
+            for off in range(1, F):
+                copy_ef(0, off).start()
+            square = squares[s]
+            for off in range(1, S):
+                copy_q(off).wait_recv()
+                square = square + sqrecv[off]
+            step_sizes = 0.5 / (1.0 + jnp.sum(square, axis=0, keepdims=True))
+        for off in range(1, Z):
+            copy_a(t, off).wait_recv()
+            copy_b(t, off).start()
+        if t == 0:
+            for off in range(1, F):
+                copy_ef(0, off).wait_recv()
+            exs[0, s] = functools.reduce(jnp.maximum, [exf[0, at] for at in range(F)])
+            for off in range(1, S):
+                copy_es(0, off).start()
+        for off in range(Z):
+            copy_b(t, off).wait_recv()
+        turn(lambda k: resid[t, 2 * k : 2 * k + 2].reshape(2 * B, K))
+        own = grad_parts(t)
+        gradient = grad_sum(t, own)
+        if t == 0:
+            for off in range(1, S):
+                copy_es(0, off).wait_recv()
+            penalty_max = top(functools.reduce(jnp.maximum, [exs[0, at] for at in range(S)]))
+            penalty = penalty_max / (8.0 + 4.0 * index[0].astype(F32))
+        grad_norms = column_norms(gradient)
+        norms[s, t : t + 1, :] = grad_norms
+        gmax_rows.append(fold(grad_norms, jnp.maximum))
+        if t < ITERS:
+            keep = mask[t : t + 1, pl.ds(pl.multiple_of(s * W, W), W)].astype(F32)
+            pruned_rows.append(fold(1.0 - keep, jnp.add))
+            moved = cur[...] + step_sizes * gradient
+            moved_norms = column_norms(moved)
+            cutoff = step_sizes * penalty
+            factor = jnp.maximum(moved_norms - cutoff, 0.0) / jnp.maximum(moved_norms, cutoff)
+            after = (keep * factor) * moved
+            cur[...] = after
+            upright = after.T
+            half[t + 1, s] = upright.astype(BF16)
+            for off in range(1, S):
+                copy_h(t + 1, off).start()
+            if t + 1 == ITERS:
+                coefs[s] = upright
+                for off in range(1, S):
+                    copy_c(off).start()
+            for off in range(1, S):
+                copy_h(t + 1, off).wait_recv()
+
+    for off in range(1, S):
+        copy_n(off).start()
+    added = [row[0] for row in sums] + [row[1] for row in sums] + bn_rows + pruned_rows
+    n_add = len(added)
+    blank = jnp.zeros((STATS - n_add - len(gmax_rows), LANES), F32)
+    exf[1, f] = jnp.concatenate(added + gmax_rows + [blank], axis=0)
+    for off in range(1, F):
+        copy_ef(1, off).start()
+
+    def merge(tiles):
+        plus = functools.reduce(jnp.add, tiles)
+        most = functools.reduce(jnp.maximum, tiles)
+        at = lax.broadcasted_iota(jnp.int32, plus.shape, 0)
+        return jnp.where(at < n_add, plus, most)
+
+    for off in range(1, F):
+        copy_ef(1, off).wait_recv()
+    exs[1, s] = merge([exf[1, at] for at in range(F)])
+    for off in range(1, S):
+        copy_es(1, off).start()
+    for off in range(1, S):
+        copy_c(off).wait_recv()
+    coef_out[...] = coefs[...].reshape(C, K)
+    for off in range(1, S):
+        copy_n(off).wait_recv()
+    for off in range(1, S):
+        copy_es(1, off).wait_recv()
+    merged = merge([exs[1, at] for at in range(S)])
+    added_up = jnp.sum(merged, axis=1, keepdims=True)
+    highest = jnp.max(merged, axis=1, keepdims=True)
+    T = ITERS + 1
+    lines = []
+    for t in range(T):
+        rr, ry, bn = (added_up[at : at + 1] for at in (t, T + t, 2 * T + t))
+        scale = jnp.maximum(penalty, highest[n_add + t : n_add + t + 1])
+        primal = 0.5 * rr + penalty * bn
+        ratio = penalty / scale
+        dual = ratio * ry - 0.5 * ratio * ratio * rr
+        lines.append((primal - dual) / (primal + 1.0))
+        for c in range(S):
+            corr_out[t : t + 1, c * W : (c + 1) * W] = norms[c, t : t + 1, :] / scale
+    for t in range(ITERS):
+        lines.append(added_up[3 * T + t : 3 * T + t + 1])
+    for at, line in enumerate(lines):
+        info_out[at : at + 1, :] = jnp.broadcast_to(line, (1, LANES))
+
+    for t in range(ITERS + 1):
+        for off in range(Z):
+            copy_y(t, off).wait_send()
+            copy_b(t, off).wait_send()
+            if off:
+                copy_z(t, off).wait_send()
+                copy_a(t, off).wait_send()
+    for off in range(1, S):
+        for t in range(ITERS + 2):
+            copy_g(t, off).wait_send()
+        for t in range(1, ITERS + 1):
+            copy_h(t, off).wait_send()
+        copy_q(off).wait_send()
+        copy_c(off).wait_send()
+        copy_n(off).wait_send()
+        copy_es(0, off).wait_send()
+        copy_es(1, off).wait_send()
+    for off in range(1, F):
+        copy_ef(0, off).wait_send()
+        copy_ef(1, off).wait_send()
+
+
+def fused(design, targets, warm_start, active_mask, penalty_index):
+    F, S = lax.axis_size("feat"), lax.axis_size("samp")
+    R, C = design.shape
+    K = targets.shape[1]
+    Z, B, W, T = F // 2, R // F, C // S, ITERS + 1
+    dma = pltpu.SemaphoreType.DMA
+    vmem = pl.BlockSpec(memory_space=pltpu.VMEM)
+    coefficients, correlations, info = pl.pallas_call(
+        functools.partial(kernel, (F, Z, S)),
+        out_shape=(
+            jax.ShapeDtypeStruct((C, K), F32),
+            jax.ShapeDtypeStruct((T, C), F32),
+            jax.ShapeDtypeStruct((8, LANES), F32),
+        ),
+        in_specs=[vmem] * 4 + [pl.BlockSpec(memory_space=pltpu.SMEM)],
+        out_specs=(vmem,) * 3,
+        scratch_shapes=[
+            pltpu.VMEM((B, K), F32),
+            pltpu.VMEM((T, Z, B, K), SHARE),
+            pltpu.VMEM((T, Z, B, K), SHARE),
+            pltpu.VMEM((T, Z, B, K), SHARE),
+            pltpu.VMEM((T, Z, B, K), SHARE),
+            pltpu.VMEM((T, F, B, K), BF16),
+            pltpu.VMEM((K, R), BF16),
+            pltpu.VMEM((T + 1, S, K, W), GRAD),
+            pltpu.VMEM((T + 1, S, K, W), GRAD),
+            pltpu.VMEM((T, S, W, K), BF16),
+            pltpu.VMEM((K, W), F32),
+            pltpu.VMEM((S, 8, W), F32),
+            pltpu.VMEM((S, 8, W), F32),
+            pltpu.VMEM((S, W, K), F32),
+            pltpu.VMEM((S, 8, W), F32),
+            pltpu.VMEM((2, F, STATS, LANES), F32),
+            pltpu.VMEM((2, S, STATS, LANES), F32),
+        ]
+        + [dma((T, Z))] * 8
+        + [dma((T + 1, S))] * 2
+        + [dma((T, S))] * 2
+        + [dma((S,))] * 6
+        + [dma((2, F))] * 2
+        + [dma((2, S))] * 2,
+        compiler_params=pltpu.CompilerParams(
+            collective_id=0, has_side_effects=True, vmem_limit_bytes=62 * 1024 * 1024
+        ),
+    )(design, targets, warm_start, active_mask, penalty_index)
+    gaps = info[: T, 0]
+    pruned = info[T : T + ITERS, 0]
+    return coefficients, correlations, gaps, pruned
 
 
 def group_norms(matrix):
@@ -16,7 +401,7 @@
     )
 
 
-def local(design, targets, warm_start, active_mask, penalty_index):
+def plain(design, targets, warm_start, active_mask, penalty_index):
     row_count, col_count = design.shape
     feat_size = lax.axis_size("feat")
     feat_slot = lax.axis_index("feat")
@@ -72,6 +457,20 @@
     return (current, jnp.stack(correlations), jnp.stack(relative_gaps), jnp.stack(pruned_counts))
 
 
+def local(design, targets, warm_start, active_mask, penalty_index):
+    feat, samp = lax.axis_size("feat"), lax.axis_size("samp")
+    rows, cols = design.shape
+    fits = (
+        feat % 2 == 0
+        and rows % (feat * 16) == 0
+        and (2 * rows // feat) % LANES == 0
+        and cols % (samp * LANES) == 0
+        and targets.shape[1] == LANES
+    )
+    form = fused if fits else plain
+    return form(design, targets, warm_start, active_mask, penalty_index)
+
+
 def solution(mesh):
     placed = (P("samp", "feat"), P("samp", None), P("feat", None), P(None, "feat"), P())
     return jax.shard_map(

time: 528 us -> 167 us (0.32)
  waiting for transfers between devices: 334 us -> 0 us
  Pallas kernels: 0 us -> 159 us
  blocking collectives: 92.5 us -> 0 us
  matrix products: 40.5 us -> 0 us
  between operations: 30.1 us -> 1.29 us
  other arithmetic: 26.4 us -> 0 us
    psum x6 -> x0, waiting for transfers between devices: 334 us -> none  [the longest x3 278 us: local(): fitted = lax.psum(fitted_part, 'feat')]
    pallas_call x0 -> x1, Pallas kernels: none -> 159 us  [fused(): pl.pallas_call(functools.partial(kernel, (F, Z, S)), out_shape=(jax.Shape...]
    psum x2 -> x0, blocking collectives: 48.9 us -> none  [the longest x1 41.8 us: local(): lax.psum((rr_local, ry_local, bn_local, pruned_local), ('feat', 'samp'))]
    pmax x2 -> x0, blocking collectives: 43.6 us -> none  [the longest x1 22 us: local(): penalty_max = lax.pmax(jnp.max(group_norms(corr_y)), 'feat')]
    dot_general x7 -> x0, matrix products: 40.5 us -> none  [the longest x4 21.2 us: transpose_product(): lax.dot_general(design, right_side, (((0,), (0,)), ((), ())), preferred_e...]
    reduce_sum x13 -> x0, other arithmetic: 15.7 us -> none  [the longest x6 6.27 us: group_norms(): return jnp.sqrt(jnp.sum(matrix * matrix, axis=1))]
  transfers between devices with their start and end apart: 6 -> 0, of which waited for: 5 -> 0; matrix products, arithmetic and copies ran while one was open for 4% -> 0% of each run, Pallas kernels for 0% -> 0%
where the time goes in v1:
time: 167 us; the launch traced here: 166 us
  Pallas kernels  159 us (95%)
  local copies, waits for them, and re-layouts  5.79 us (3%)
    pallas_call x1, Pallas kernels, fused(): pl.pallas_call(functools.partial(kernel, (F, Z, S)), out_shape=(jax.Shape...  159 us

profile of v1, /device:TPU:0, one launch (start us, length us, event | category | flops | bytes accessed | tf_op | source)
XLA Modules:
  0.0 166.4 jit_solution(16437273071391600128)
XLA Ops:
  1.3 159.3 %shard_map.84 = (f32[1024,128]{1,0:T(8,128)}, f32[3,1024]{1,0:T(4,128)}, f32[8,128]{1,0:T(8,128)}) custom-call(bf16[3584,1024]{1,0:T(8,128)(2,1)} %design.1, bf16[3584,128]{1,0:T(8,128)(2,1)} %targets.1, f32[1024,128]{1,0:T(8,128)} %warm.1, s32[2,1024]{1,0:T(2,128)} %mask.1, s32[1]{0:T(128)S(6)} %copy.11.index), custom_call_target="tpu_custom_call" | custom-call | tf_op jit(solution)/shard_map/pallas_call | solution.py:351
  160.6 1.3 slice_reduce_fusion
  161.9 1.3 slice_reduce_fusion.1
  163.2 1.9 %copy.12 = f32[1024,128]{1,0:T(8,128)} copy(f32[1024,128]{1,0:T(8,128)} %get-tuple-element.14) | data formatting | bytes 1048576
  165.0 1.3 copy.13

commit v2 on v1

--- a/solution.py
+++ b/solution.py
@@ -12,7 +12,8 @@
 BF16 = jnp.bfloat16
 LANES = 128
 SHARE = BF16
-GRAD = F32
+GRAD = BF16
+H = 2
 STATS = 16
 
 
@@ -34,17 +35,18 @@
 
 
 def kernel(
-    sizes, design, targets, warm, mask, index, coef_out, corr_out, info_out,
-    mine, ysend, yrecv, zsend, zrecv, resid, turned, gsend, grecv, half, cur, squares,
+    sizes, stored, targets, warm, mask, index, coef_out, corr_out, info_out,
+    design, gacc, mine, ysend, yrecv, zsend, zrecv, resid, turned, gsend, grecv, half, cur, squares,
     sqrecv, coefs, norms, exf, exs,
     y_s, y_r, z_s, z_r, a_s, a_r, b_s, b_r, g_s, g_r, h_s, h_r, q_s, q_r, c_s, c_r, n_s, n_r,
-    ef_s, ef_r, es_s, es_r,
+    ef_s, ef_r, es_s, es_r, d_s,
 ):
     F, Z, S = sizes
     R, C = design.shape
     K = targets.shape[1]
     B = R // F
     W = C // S
+    b = B // H
     f = lax.axis_index("feat")
     s = lax.axis_index("samp")
     z, y = f // 2, lax.rem(f, 2)
@@ -71,22 +73,33 @@
             device_id={"samp": ahead_s(off)}, device_id_type=pl.DeviceIdType.MESH,
         )
 
-    def copy_y(t, off):
-        return feat_copy(ysend.at[t, off], yrecv.at[t, off], y_s.at[t, off], y_r.at[t, off], partner)
-
-    def copy_z(t, off):
-        return feat_copy(
-            zsend.at[t, off], zrecv.at[t, off], z_s.at[t, off], z_r.at[t, off], ahead_z(off) * 2 + y
-        )
-
-    def copy_a(t, off):
-        return feat_copy(
-            resid.at[t, f], resid.at[t, f], a_s.at[t, off], a_r.at[t, off], ahead_z(off) * 2 + y
-        )
-
-    def copy_b(t, off):
-        slot = behind_z(off) * 2 + y
-        return feat_copy(resid.at[t, slot], resid.at[t, slot], b_s.at[t, off], b_r.at[t, off], partner)
+    def rows_of(slot):
+        return pl.ds(pl.multiple_of(slot * B, B), B)
+
+    def half_of(slot, h):
+        return pl.ds(pl.multiple_of(slot * B + h * b, b), b)
+
+    def copy_d(own, off):
+        at = rows_of(ahead_z(off) * 2 + (y if own else 1 - y))
+        return pltpu.make_async_copy(stored.at[at, :], design.at[at, :], d_s.at[own, off])
+
+    def copy_y(t, off, h):
+        at = (t, off, h)
+        return feat_copy(ysend.at[at], yrecv.at[at], y_s.at[at], y_r.at[at], partner)
+
+    def copy_z(t, off, h):
+        at = (t, off, h)
+        return feat_copy(zsend.at[at], zrecv.at[at], z_s.at[at], z_r.at[at], ahead_z(off) * 2 + y)
+
+    def copy_a(t, off, h):
+        at = (t, off, h)
+        own = resid.at[t, f, h]
+        return feat_copy(own, own, a_s.at[at], a_r.at[at], ahead_z(off) * 2 + y)
+
+    def copy_b(t, off, h):
+        at = (t, off, h)
+        block = resid.at[t, behind_z(off) * 2 + y, h]
+        return feat_copy(block, block, b_s.at[at], b_r.at[at], partner)
 
     def copy_g(t, off):
         return samp_copy(gsend.at[t, off], grecv.at[t, off], g_s.at[t, off], g_r.at[t, off], off)
@@ -118,6 +131,9 @@
 
         lax.fori_loop(first, count, step, 0)
 
+    for own in range(2):
+        for i in range(Z):
+            copy_d(own, (i + 1) % Z).start()
     barrier = pltpu.get_barrier_semaphore()
     for off in range(1, F):
         pl.semaphore_signal(
@@ -133,29 +149,28 @@
     cur[...] = warm[pl.ds(pl.multiple_of(s * W, W), W), :].T
     pl.semaphore_wait(barrier, F - 1 + S - 1)
 
-    def rows_of(slot):
-        return pl.ds(pl.multiple_of(slot * B, B), B)
-
-    def share(t, slot):
-        return jnp.dot(design[rows_of(slot), :], half[t].reshape(C, K), preferred_element_type=F32)
-
-    def turn(source):
-        step = 2 * B
-        for k in range(Z):
-            turned[:, k * step : (k + 1) * step] = source(k).T
-
-    def grad_parts(t):
+    def share(t, slot, h):
+        block = design[half_of(slot, h), :]
+        return jnp.dot(block, half[t].reshape(C, K), preferred_element_type=F32)
+
+    def grad_chunk(t, k, chunk, first, last):
+        turned[...] = chunk.T
+        rows = pl.ds(pl.multiple_of(k * 2 * B, 2 * B), 2 * B)
+
         def part(off):
             at = pl.ds(pl.multiple_of(ahead_s(off) * W, W), W)
-            return jnp.dot(turned[...], design[:, at], preferred_element_type=F32)
-
-        def send(off):
-            gsend[t, off] = part(off).astype(GRAD)
-            copy_g(t, off).start()
-
-        each(S, send, 1)
-        gsend_own = part(0)
-        return gsend_own
+            piece = jnp.dot(turned[...], design[rows, at], preferred_element_type=F32)
+            return piece if first else gacc[off] + piece
+
+        def step(off):
+            if last:
+                gsend[t, off] = part(off).astype(GRAD)
+                copy_g(t, off).start()
+            else:
+                gacc[off] = part(off)
+
+        each(S, step, 1)
+        gacc[0] = part(0)
 
     def grad_sum(t, own):
         for off in range(1, S):
@@ -184,43 +199,54 @@
     for t in range(ITERS + 1):
         bn_rows.append(fold(column_norms(cur[...]), jnp.add))
 
-        def send_y(i):
-            off = lax.rem(i + 1, Z)
-            ysend[t, off] = share(t, ahead_z(off) * 2 + 1 - y).astype(SHARE)
-            copy_y(t, off).start()
-
-        each(Z, send_y)
-
-        def send_z(off):
-            mine[...] = share(t, ahead_z(off) * 2 + y)
-            copy_y(t, off).wait_recv()
-            zsend[t, off] = (mine[...] + yrecv[t, off].astype(F32)).astype(SHARE)
-            copy_z(t, off).start()
-
-        each(Z, send_z, 1)
-        mine[...] = share(t, f)
+        for h in range(H):
+
+            def send_y(i):
+                off = lax.rem(i + 1, Z)
+                if t == 0 and h == 0:
+                    copy_d(0, off).wait()
+                ysend[t, off, h] = share(t, ahead_z(off) * 2 + 1 - y, h).astype(SHARE)
+                copy_y(t, off, h).start()
+
+            each(Z, send_y)
+
+        for h in range(H):
+
+            def send_z(off):
+                if t == 0 and h == 0:
+                    copy_d(1, off).wait()
+                mine[...] = share(t, ahead_z(off) * 2 + y, h)
+                copy_y(t, off, h).wait_recv()
+                zsend[t, off, h] = (mine[...] + yrecv[t, off, h].astype(F32)).astype(SHARE)
+                copy_z(t, off, h).start()
+
+            each(Z, send_z, 1)
         if t == 0:
-            turn(lambda k: targets[k * 2 * B : (k + 1) * 2 * B, :])
-            corr_own = grad_parts(ITERS + 1)
+            copy_d(1, 0).wait()
+            for k in range(Z):
+                chunk = targets[k * 2 * B : (k + 1) * 2 * B, :]
+                grad_chunk(ITERS + 1, k, chunk, k == 0, k == Z - 1)
+            corr_own = gacc[0]
             square_columns()
-        copy_y(t, 0).wait_recv()
-        fitted = mine[...] + yrecv[t, 0].astype(F32)
-        for off in range(1, Z):
-            copy_z(t, off).wait_recv()
-            fitted = fitted + zrecv[t, off].astype(F32)
-        own_targets = targets[rows_of(f), :].astype(F32)
-        rounded = (own_targets - fitted).astype(BF16)
-        resid[t, f] = rounded
-        for off in range(1, Z):
-            copy_a(t, off).start()
-        copy_b(t, 0).start()
-        wide = rounded.astype(F32)
-        sums.append(
-            (
-                jnp.sum(wide * wide, axis=0, keepdims=True),
-                jnp.sum(wide * own_targets, axis=0, keepdims=True),
-            )
-        )
+        rr = jnp.zeros((1, K), F32)
+        ry = jnp.zeros((1, K), F32)
+        for h in range(H):
+            fitted = share(t, f, h)
+            copy_y(t, 0, h).wait_recv()
+            fitted = fitted + yrecv[t, 0, h].astype(F32)
+            for off in range(1, Z):
+                copy_z(t, off, h).wait_recv()
+                fitted = fitted + zrecv[t, off, h].astype(F32)
+            own_targets = targets[half_of(f, h), :].astype(F32)
+            rounded = (own_targets - fitted).astype(BF16)
+            resid[t, f, h] = rounded
+            for off in range(1, Z):
+                copy_a(t, off, h).start()
+            copy_b(t, 0, h).start()
+            wide = rounded.astype(F32)
+            rr = rr + jnp.sum(wide * wide, axis=0, keepdims=True)
+            ry = ry + jnp.sum(wide * own_targets, axis=0, keepdims=True)
+        sums.append((rr, ry))
         if t == 0:
             corr = grad_sum(ITERS + 1, corr_own)
             exf[0, f] = jnp.broadcast_to(fold(column_norms(corr), jnp.maximum), (STATS, LANES))
@@ -231,9 +257,6 @@
                 copy_q(off).wait_recv()
                 square = square + sqrecv[off]
             step_sizes = 0.5 / (1.0 + jnp.sum(square, axis=0, keepdims=True))
-        for off in range(1, Z):
-            copy_a(t, off).wait_recv()
-            copy_b(t, off).start()
         if t == 0:
             for off in range(1, F):
                 copy_ef(0, off).wait_recv()
@@ -241,10 +264,16 @@
             for off in range(1, S):
                 copy_es(0, off).start()
         for off in range(Z):
-            copy_b(t, off).wait_recv()
-        turn(lambda k: resid[t, 2 * k : 2 * k + 2].reshape(2 * B, K))
-        own = grad_parts(t)
-        gradient = grad_sum(t, own)
+            if off + 1 < Z:
+                for h in range(H):
+                    copy_a(t, off + 1, h).wait_recv()
+                    copy_b(t, off + 1, h).start()
+            for h in range(H):
+                copy_b(t, off, h).wait_recv()
+            k = behind_z(off)
+            chunk = resid[t, pl.ds(2 * k, 2)].reshape(2 * B, K)
+            grad_chunk(t, k, chunk, off == 0, off == Z - 1)
+        gradient = grad_sum(t, gacc[0])
         if t == 0:
             for off in range(1, S):
                 copy_es(0, off).wait_recv()
@@ -320,12 +349,18 @@
         info_out[at : at + 1, :] = jnp.broadcast_to(line, (1, LANES))
 
     for t in range(ITERS + 1):
-        for off in range(Z):
-            copy_y(t, off).wait_send()
-            copy_b(t, off).wait_send()
-            if off:
-                copy_z(t, off).wait_send()
-                copy_a(t, off).wait_send()
+        for h in range(H):
+
+            def drain(off):
+                copy_y(t, off, h).wait_send()
+                copy_b(t, off, h).wait_send()
+
+            def drain_line(off):
+                copy_z(t, off, h).wait_send()
+                copy_a(t, off, h).wait_send()
+
+            each(Z, drain)
+            each(Z, drain_line, 1)
     for off in range(1, S):
         for t in range(ITERS + 2):
             copy_g(t, off).wait_send()
@@ -339,6 +374,15 @@
     for off in range(1, F):
         copy_ef(0, off).wait_send()
         copy_ef(1, off).wait_send()
+
+
+def finish(coef, corr, info, coef_out, corr_out, gaps_out, pruned_out):
+    coef_out[...] = coef[...]
+    corr_out[...] = corr[...]
+    for at in range(ITERS + 1):
+        gaps_out[at] = info[at, 0]
+    for at in range(ITERS):
+        pruned_out[at] = info[ITERS + 1 + at, 0]
 
 
 def fused(design, targets, warm_start, active_mask, penalty_index):
@@ -355,16 +399,18 @@
             jax.ShapeDtypeStruct((T, C), F32),
             jax.ShapeDtypeStruct((8, LANES), F32),
         ),
-        in_specs=[vmem] * 4 + [pl.BlockSpec(memory_space=pltpu.SMEM)],
+        in_specs=[pl.BlockSpec(memory_space=pl.ANY)] + [vmem] * 3 + [pl.BlockSpec(memory_space=pltpu.SMEM)],
         out_specs=(vmem,) * 3,
         scratch_shapes=[
-            pltpu.VMEM((B, K), F32),
-            pltpu.VMEM((T, Z, B, K), SHARE),
-            pltpu.VMEM((T, Z, B, K), SHARE),
-            pltpu.VMEM((T, Z, B, K), SHARE),
-            pltpu.VMEM((T, Z, B, K), SHARE),
-            pltpu.VMEM((T, F, B, K), BF16),
-            pltpu.VMEM((K, R), BF16),
+            pltpu.VMEM((R, C), BF16),
+            pltpu.VMEM((S, K, W), F32),
+            pltpu.VMEM((B // H, K), F32),
+            pltpu.VMEM((T, Z, H, B // H, K), SHARE),
+            pltpu.VMEM((T, Z, H, B // H, K), SHARE),
+            pltpu.VMEM((T, Z, H, B // H, K), SHARE),
+            pltpu.VMEM((T, Z, H, B // H, K), SHARE),
+            pltpu.VMEM((T, F, H, B // H, K), BF16),
+            pltpu.VMEM((K, 2 * B), BF16),
             pltpu.VMEM((T + 1, S, K, W), GRAD),
             pltpu.VMEM((T + 1, S, K, W), GRAD),
             pltpu.VMEM((T, S, W, K), BF16),
@@ -376,19 +422,29 @@
             pltpu.VMEM((2, F, STATS, LANES), F32),
             pltpu.VMEM((2, S, STATS, LANES), F32),
         ]
-        + [dma((T, Z))] * 8
+        + [dma((T, Z, H))] * 8
         + [dma((T + 1, S))] * 2
         + [dma((T, S))] * 2
         + [dma((S,))] * 6
         + [dma((2, F))] * 2
-        + [dma((2, S))] * 2,
+        + [dma((2, S))] * 2
+        + [dma((2, Z))],
         compiler_params=pltpu.CompilerParams(
             collective_id=0, has_side_effects=True, vmem_limit_bytes=62 * 1024 * 1024
         ),
     )(design, targets, warm_start, active_mask, penalty_index)
-    gaps = info[: T, 0]
-    pruned = info[T : T + ITERS, 0]
-    return coefficients, correlations, gaps, pruned
+    smem = pl.BlockSpec(memory_space=pltpu.SMEM)
+    return pl.pallas_call(
+        finish,
+        out_shape=(
+            jax.ShapeDtypeStruct((C, K), F32),
+            jax.ShapeDtypeStruct((T, C), F32),
+            jax.ShapeDtypeStruct((T,), F32),
+            jax.ShapeDtypeStruct((ITERS,), F32),
+        ),
+        in_specs=[vmem, vmem, smem],
+        out_specs=(vmem, vmem, smem, smem),
+    )(coefficients, correlations, info)
 
 
 def group_norms(matrix):
@@ -462,7 +518,7 @@
     rows, cols = design.shape
     fits = (
         feat % 2 == 0
-        and rows % (feat * 16) == 0
+        and rows % (feat * 16 * H) == 0
         and (2 * rows // feat) % LANES == 0
         and cols % (samp * LANES) == 0
         and targets.shape[1] == LANES

time: 167 us -> 144 us (0.86)
  Pallas kernels: 159 us -> 143 us
  local copies, waits for them, and re-layouts: 5.79 us -> 0 us
    pallas_call x1, Pallas kernels: 159 us -> 141 us  [fused(): pl.pallas_call(functools.partial(kernel, (F, Z, S)), out_shape=(jax.Shape...]
    unnamed x2 -> x0, local copies, waits for them, and re-layouts: 3.19 us -> none
    slice x2 -> x0, local copies, waits for them, and re-layouts: 2.6 us -> none  [the longest x1 1.3 us: fused(): gaps = info[:T, 0]]
    pallas_call x0 -> x1, Pallas kernels: none -> 1.9 us  [fused(): pl.pallas_call(finish, out_shape=(jax.ShapeDtypeStruct((C, K), F32), jax....]
where the time goes in v2:
time: 144 us
  Pallas kernels  143 us (99%)
    pallas_call x1, Pallas kernels, fused(): pl.pallas_call(functools.partial(kernel, (F, Z, S)), out_shape=(jax.Shape...  141 us

profile of v2, /device:TPU:0, one launch (start us, length us, event | category | flops | bytes accessed | tf_op | source)
XLA Modules:
  0.0 144.0 jit_solution(5995849915453493894)
XLA Ops:
  1.3 140.8 %shard_map.84 = (f32[1024,128]{1,0:T(8,128)}, f32[3,1024]{1,0:T(4,128)}, f32[8,128]{1,0:T(8,128)}) custom-call(bf16[3584,1024]{1,0:T(8,128)(2,1)} %stored.1, bf16[3584,128]{1,0:T(8,128)(2,1)} %targets.1, f32[1024,128]{1,0:T(8,128)} %warm.1, s32[2,1024]{1,0:T(2,128)} %mask.1, s32[1]{0:T(128)S(6)} %copy.9.index), custom_call_target="tpu_custom_call" | custom-call | tf_op jit(solution)/shard_map/pallas_call | solution.py:395
  142.1 1.9 %shard_map.85 = (f32[1024,128]{1,0:T(8,128)}, f32[3,1024]{1,0:T(4,128)}, f32[3]{0:T(128)}, f32[2]{0:T(128)}) custom-call(f32[1024,128]{1,0:T(8,128)} %get-tuple-element.7.coef, f32[3,1024]{1,0:T(4,128)} %get-tuple-element.8.corr, f32[8,128]{1,0:T(8,128)} %get-tuple-element.9.info), custom_call_target="tpu_custom_call" | custom-call | tf_op jit(solution)/shard_map/pallas_call | solution.py:437
